TPU v7x, 32 devices: a whole 2x2x4 slice. The times are simulated.
32 devices in a mesh: tm: 8 (over y, x, core), sr: 4 (over z).
Axes of the slice: x: 2, y: 2, z: 4, core: 2. Of those that a mesh axis runs over, the one named last changes fastest.
Arguments:
- observations: bfloat16 [1024, 65536], P(None, ('sr', 'tm')), may hold values from -6 to 6
- loadings: float32 [65536, 128], P(('sr', 'tm')), may hold values from -0.0007324219 to 0.0007324219
- noise_precision: float32 [65536], P(('sr', 'tm')), may hold values from 0.5 to 4
- transition: float32 [128, 128], replicated, may hold values from -1 to 1, as said below
- filter_cov: float32 [128, 128], replicated, may hold values from -1 to 1, as said below
- smoother_gain: float32 [128, 128], replicated, may hold values from -1 to 1, as said below
- smoothed_cov: float32 [128, 128], replicated, may hold values from -1 to 1, as said below
Outputs:
- smoothed_factors: float32 [1024, 128], P('tm')
- new_loadings: float32 [65536, 128], P(('sr', 'tm'))
- new_transition: float32 [128, 128], replicated
Inputs may be any that keep to these rules, and one draw needn't show every extreme that they name: `transition`: the spectral radius is below one. `filter_cov`: symmetric positive definite. `smoother_gain`: the spectral radius is below one. `smoothed_cov`: symmetric positive definite.
All inputs are finite; a program needn't handle non-finite values.
Results may differ from a plain program's by a relative error of at most 0.00175.
The roundings to bfloat16 on the way count: a program that leaves them out, or rounds other values in their place, can miss the bound.
Values may be sent and summed in bfloat16 or wider, within the bound.
A program may use at most 64 MiB of HBM per device.

v0:
```python
import jax
import jax.numpy as jnp
from jax import lax
from jax.sharding import PartitionSpec as P

precise = lax.Precision.HIGHEST


def carried_in(part, axis, combine, identity, reverse):
    count = lax.axis_size(axis)
    place = lax.axis_index(axis)
    ahead = count - 1 - place if reverse else place
    gathered = jax.tree.map(lambda a: lax.all_gather(a, axis), part)
    state = jax.tree.map(lambda a, e: jnp.zeros_like(a) + jnp.asarray(e, a.dtype), part, identity)

    def one(hop, state):
        source = count - 1 - hop if reverse else hop
        return combine(
            state, jax.tree.map(lambda a: lax.dynamic_index_in_dim(a, source, 0, False), gathered)
        )

    return lax.fori_loop(0, ahead, one, state)


def shifted(value, axis, steps):
    count = lax.axis_size(axis)
    leading, last = (max(0, -steps), min(count, count - steps))
    return lax.ppermute(value, axis, [(source, source + steps) for source in range(leading, last)])


def dot_high(left, right):
    return jnp.dot(left, right, precision=precise, preferred_element_type=jnp.float32)


def matrix_power(matrix, exponent):
    result = jnp.eye(matrix.shape[0], dtype=jnp.float32)
    square = matrix
    remain = exponent
    while remain > 0:
        if remain % 2 == 1:
            result = dot_high(result, square)
        remain = remain // 2
        if remain > 0:
            square = dot_high(square, square)
    return result


def block_prefix(inputs, matrix):
    length = inputs.shape[0]
    width = inputs.shape[1]
    totals = inputs
    raised = matrix
    offset = 1
    while offset < length:
        moved = jnp.concatenate(
            [jnp.zeros((offset, width), jnp.float32), totals[: length - offset]], axis=0
        )
        totals = totals + dot_high(moved, raised.T)
        offset = offset * 2
        if offset < length:
            raised = dot_high(raised, raised)
    return totals


def propagate(start, matrix, length):
    carried = dot_high(matrix, start)[None, :]
    raised = matrix
    while carried.shape[0] < length:
        carried = jnp.concatenate([carried, dot_high(carried, raised.T)], axis=0)
        raised = dot_high(raised, raised)
    return carried


def compose(earlier, later):
    return (dot_high(later[0], earlier[0]), dot_high(later[0], earlier[1]) + later[1])


def local(
    observations, loadings, noise_precision, transition, filter_cov, smoother_gain, smoothed_cov
):
    blocks = lax.axis_size("tm")
    position = lax.axis_index("tm")
    width = transition.shape[0]
    steps_dev = observations.shape[0] // blocks
    scaled = (noise_precision[:, None] * loadings).astype(jnp.bfloat16)
    window = observations
    partial_value = lax.psum_scatter(
        jnp.dot(window, scaled, preferred_element_type=jnp.float32),
        "tm",
        scatter_dimension=0,
        tiled=True,
    )
    info_part = dot_high(loadings.T, noise_precision[:, None] * loadings)
    proj = lax.psum(partial_value, "sr")
    info = lax.psum(info_part, ("tm", "sr"))
    closed = transition - dot_high(filter_cov, dot_high(info, transition))
    inputs = dot_high(proj, filter_cov.T)
    local_filter = block_prefix(inputs, closed)
    whole_filter = matrix_power(closed, steps_dev)
    identity_pair = (jnp.eye(width, dtype=jnp.float32), jnp.zeros((width,), jnp.float32))
    entering = carried_in(
        (whole_filter, local_filter[steps_dev - 1]), "tm", compose, identity_pair, False
    )[1]
    filtered = local_filter + propagate(entering, closed, steps_dev)
    coupled = dot_high(smoother_gain, transition)
    global_rows = position * steps_dev + jnp.arange(steps_dev, dtype=jnp.int32)
    final_row = (global_rows == steps_dev * blocks - 1)[:, None]
    back = jnp.where(final_row, filtered, filtered - dot_high(filtered, coupled.T))
    local_smooth = block_prefix(back[::-1], smoother_gain)[::-1]
    whole_smooth = matrix_power(smoother_gain, steps_dev)
    arriving = carried_in((whole_smooth, local_smooth[0]), "tm", compose, identity_pair, True)[1]
    smoothed = local_smooth + propagate(arriving, smoother_gain, steps_dev)[::-1]
    factors_b = smoothed.astype(jnp.bfloat16)
    prior_row = shifted(smoothed[steps_dev - 1 :], "tm", 1)
    lag_rows = jnp.concatenate([prior_row, smoothed[: steps_dev - 1]], axis=0)
    kept_rows = jnp.where(final_row, 0.0, smoothed)
    total_part = dot_high(smoothed.T, smoothed)
    previous_part = dot_high(kept_rows.T, kept_rows)
    lagged_part = dot_high(smoothed.T, lag_rows)
    total, previous, lagged = lax.psum((total_part, previous_part, lagged_part), "tm")
    length = steps_dev * blocks
    total = total + length * smoothed_cov
    previous = previous + (length - 1) * smoothed_cov
    lagged = lagged + (length - 1) * dot_high(smoothed_cov, smoother_gain.T)
    window = observations
    cross = jnp.einsum(
        "ts,tk->sk",
        window,
        lax.all_gather(factors_b, "tm", axis=0, tiled=True),
        preferred_element_type=jnp.float32,
    )
    total_factor = jnp.linalg.cholesky(total)
    new_loadings = jax.scipy.linalg.cho_solve((total_factor, True), cross.T).T
    previous_factor = jnp.linalg.cholesky(previous)
    new_transition = jax.scipy.linalg.cho_solve((previous_factor, True), lagged.T).T
    return (smoothed, new_loadings, new_transition)


def solution(mesh):
    in_specs = (P(None, ("sr", "tm")), P(("sr", "tm"), None), P(("sr", "tm")), P(), P(), P(), P())
    out_specs = (P("tm", None), P(("sr", "tm"), None), P())
    return jax.shard_map(local, mesh=mesh, in_specs=in_specs, out_specs=out_specs, check_vma=False)
```

profile of v0, /device:TPU:0, one launch (start us, length us, event | category | flops | bytes accessed | tf_op | source)
XLA Modules:
  0.0 331.9 jit_solution(2547815003200978211)
XLA Ops:
  8.1 4.4 %fusion.13 = f32[128,128]{0,1:T(8,128)} fusion(f32[2048,128]{1,0:T(8,128)} %param.13, f32[2048]{0:T(1024)} %param.14), kind=kOutput, calls=%fused_computation.18 | convolution fusion | flops 402915328 | bytes 1122304 | tf_op jit(solution)/shard_map/dot_general | solution.py:32
  12.6 5.3 %convolution_bitcast_fusion.2 = f32[1024,128]{0,1:T(8,128)} fusion(bf16[1024,2048]{1,0:T(8,128)(2,1)} %param.12, f32[2048,128]{1,0:T(8,128)} %param.13, f32[2048]{0:T(1024)} %param.14), kind=kOutput, calls=%fused_computation.15 | convolution fusion | flops 537395200 | bytes 5775360 | tf_op jit(solution)/shard_map/dot_general | solution.py:88
  18.0 0.2 fusion.136
  18.6 0.3 convolution_multiply_fusion
  20.3 11.4 %all-gather.1 = f32[1024,128]{1,0:T(8,128)S(1)} all-gather(f32[128,128]{1,0:T(8,128)S(1)} %fusion.46), channel_id=3, replica_groups=mesh['tm'=8,'sr'=4] {'tm'}, dimensions={0}, use_global_device_ids=true | all-gather | bytes 589824 | tf_op jit(solution)/shard_map/all_gather | solution.py:13
  31.7 105.7 %all-reduce.21.cloned.1.call-done = f32[128,128]{0,1:T(8,128)} async-done(((f32[128,128]{0,1:T(8,128)}), f32[128,128]{0,1:T(8,128)}) %all-reduce.21.cloned.1.call-update) | async-done | bytes 65552 | tf_op jit(solution)/shard_map/psum | solution.py:95
  137.3 1.1 fusion.125
  138.5 0.3 fusion.16
  138.8 0.3 fusion.126
  140.6 10.4 %all-gather = f32[1024,128]{1,0:T(8,128)S(1)} all-gather(f32[128,128]{1,0:T(8,128)S(1)} %fusion.47), channel_id=2, replica_groups=mesh['tm'=8,'sr'=4] {'tm'}, dimensions={0}, use_global_device_ids=true | all-gather | bytes 589824 | tf_op jit(solution)/shard_map/all_gather | solution.py:13
  151.0 25.0 %all-reduce.19.cloned.1.call-done = f32[128,128]{0,1:T(8,128)} async-done(((f32[128,128]{0,1:T(8,128)}), f32[128,128]{0,1:T(8,128)}) %all-reduce.19.cloned.1.call-update) | async-done | bytes 65552 | tf_op jit(solution)/shard_map/psum | solution.py:94
  176.0 1.1 fusion.124
  177.3 0.3 convolution_add_fusion.12
  177.6 0.3 convolution_add_fusion.11
  177.8 0.3 convolution_add_fusion.10
  178.1 0.3 convolution_add_fusion.9
  178.4 0.3 convolution_add_fusion.8
  178.7 0.3 convolution_add_fusion.7
  179.0 8.8 %all-gather.2 = f32[8,1,128]{2,1,0:T(1,128)S(1)} all-gather(f32[1,1,128]{2,1,0:T(1,128)S(1)} %slice_bitcast_fusion.1), channel_id=1, replica_groups=mesh['tm'=8,'sr'=4] {'tm'}, dimensions={0}, use_global_device_ids=true | all-gather | bytes 4608 | tf_op jit(solution)/shard_map/all_gather | solution.py:13
  188.2 0.2 fusion.73
  188.5 0.2 fusion.57
  189.3 0.2 fusion.135
  189.5 0.3 fusion.12
  189.9 0.3 convolution_add_fusion.6
  190.1 0.3 convolution_add_fusion.5
  190.4 0.3 convolution_add_fusion.4
  190.7 0.3 convolution_add_fusion.3
  191.0 0.3 convolution_add_fusion.2
  191.3 0.3 convolution_add_fusion.1
  191.5 0.3 convolution_add_fusion
  191.8 9.7 %all-gather.3 = f32[8,1,128]{2,1,0:T(1,128)S(1)} all-gather(f32[1,1,128]{2,1,0:T(1,128)S(1)} %slice_bitcast_fusion), channel_id=1, replica_groups=mesh['tm'=8,'sr'=4] {'tm'}, dimensions={0}, use_global_device_ids=true | all-gather | bytes 4608 | tf_op jit(solution)/shard_map/all_gather | solution.py:13
  201.5 1.6 while.27
  201.7 0.2 fusion.247
  201.9 0.2 fusion.247
  202.2 0.2 fusion.247
  202.4 0.2 fusion.247
  202.6 0.2 fusion.247
  202.8 0.2 fusion.247
  203.1 0.2 fusion.95
  203.3 0.2 fusion.93
  203.5 0.2 fusion.89
  203.7 0.2 fusion.79
  204.0 0.2 fusion.65
  204.8 0.2 fusion.146
  205.1 1.0 fusion.36
  206.1 0.9 fusion.147
  207.0 2.0 collective-permute-start
  209.0 8.7 %all_gather.27 = bf16[1024,128]{1,0:T(8,128)(2,1)S(1)} all-gather(bf16[128,128]{1,0:T(8,128)(2,1)S(1)} %get-tuple-element.157), channel_id=1, replica_groups=mesh['tm'=8,'sr'=4] {'tm'}, dimensions={0}, use_global_device_ids=true | all-gather | bytes 294912 | tf_op jit(solution)/shard_map/all_gather | solution.py:129
  217.7 0.9 fusion.21
  218.7 2.9 fusion.148
  221.6 49.8 %all-reduce.23.cloned.1.call-done = (f32[128,128]{0,1:T(8,128)}, f32[128,128]{0,1:T(8,128)}, f32[128,128]{0,1:T(8,128)}) async-done(((f32[128,128]{0,1:T(8,128)}, f32[128,128]{0,1:T(8,128)}, f32[128,128]{0,1:T(8,128)}), (f32[128,128]{0,1:T(8,128)}, f32[128,128]{0,1:T(8,128)}, f32[128,128]{0,1:T(8,128)})) %all-reduce.23.cloned.1.call-update) | async-done | bytes 196624 | tf_op jit(solution)/shard_map/psum | solution.py:120
  271.4 0.9 multiply_add_fusion
  272.5 11.7 %cholesky.55 = f32[128,128]{1,0:T(8,128)S(1)} custom-call(f32[128,128]{1,0:T(8,128)S(1)} %get-tuple-element.161), custom_call_target="Cholesky" | custom-call | tf_op jit(solution)/shard_map/jit(cholesky)/cholesky | solution.py:134
  284.3 0.6 compare_reduce_fusion
  284.9 0.7 fusion.20
  285.6 9.8 %custom-call.17 = f32[1,128,128]{1,2,0:T(8,128)S(1)} custom-call(f32[1,128,128]{2,1,0:T(8,128)S(1)} %fusion.20), custom_call_target="InvertDiagBlocksLowerTriangular" | custom-call | tf_op jit(solution)/shard_map/jit(_cho_solve)/triangular_solve | solution.py:135
  295.4 1.1 fusion.27
  296.5 0.9 fusion.25
  297.4 11.7 %cholesky.44 = f32[128,128]{1,0:T(8,128)S(1)} custom-call(f32[128,128]{1,0:T(8,128)S(1)} %get-tuple-element.162), custom_call_target="Cholesky" | custom-call | tf_op jit(solution)/shard_map/jit(cholesky)/cholesky | solution.py:132
  309.2 0.6 compare_reduce_fusion.1
  309.8 0.7 fusion.19
  310.5 9.9 %custom-call.16 = f32[1,128,128]{1,2,0:T(8,128)S(1)} custom-call(f32[1,128,128]{2,1,0:T(8,128)S(1)} %fusion.19), custom_call_target="InvertDiagBlocksLowerTriangular" | custom-call | tf_op jit(solution)/shard_map/jit(_cho_solve)/triangular_solve | solution.py:133
  320.5 1.1 fusion.32
  321.5 2.8 fusion.30
  (87 shorter events, 6.0 us)
Async XLA Ops:
  8.0 10.0 %copy-start = (f32[128,128]{1,0:T(8,128)S(1)}, f32[128,128]{1,0:T(8,128)}, u32[]{:S(2)}) copy-start(f32[128,128]{1,0:T(8,128)} %param.17) | copy-start | bytes 196612
  8.0 9.9 %copy-start.2 = (f32[128,128]{1,0:T(8,128)S(1)}, f32[128,128]{1,0:T(8,128)}, u32[]{:S(2)}) copy-start(f32[128,128]{1,0:T(8,128)} %param.15) | copy-start | bytes 196612
  8.0 10.4 %copy-start.3 = (f32[128,128]{1,0:T(8,128)S(1)}, f32[128,128]{1,0:T(8,128)}, u32[]{:S(2)}) copy-start(f32[128,128]{1,0:T(8,128)} %param.18) | copy-start | bytes 196612
  8.0 129.3 %all-reduce.21.cloned.1.call-start = ((), (), s32[]{:S(2)}) async-start(), calls=%async_computation.3 | async-start | bytes 131072 | tf_op jit(solution)/shard_map/psum | solution.py:95
  12.5 126.0 %copy-start.4 = (f32[128,128]{1,0:T(8,128)S(1)}, f32[128,128]{1,0:T(8,128)}, u32[]{:S(2)}) copy-start(f32[128,128]{1,0:T(8,128)} %param.16) | copy-start | bytes 196612
  12.5 128.0 %reduce-scatter.2.cloned.1.call-start = ((), (), s32[]{:S(2)}) async-start(), calls=%async_computation.1 | async-start | bytes 589824 | tf_op jit(solution)/shard_map/reduce_scatter | solution.py:87
  17.9 158.1 %all-reduce.19.cloned.1.call-start = ((), (), s32[]{:S(2)}) async-start(), calls=%async_computation.2 | async-start | bytes 131072 | tf_op jit(solution)/shard_map/psum | solution.py:94
  140.6 130.9 %all-reduce.23.cloned.1.call-start = ((), (), s32[]{:S(2)}) async-start(), calls=%async_computation.4 | async-start | bytes 393216 | tf_op jit(solution)/shard_map/psum | solution.py:120
  205.1 105.4 %copy-start.1 = (f32[128,128]{1,0:T(8,128)}, f32[128,128]{1,0:T(8,128)S(1)}, u32[]{:S(2)}) copy-start(f32[128,128]{1,0:T(8,128)S(1)} %get-tuple-element.158) | copy-start | bytes 196612
  207.0 10.7 %collective-permute-start = (f32[1,128]{1,0:T(1,128)S(1)}, f32[1,128]{1,0:T(1,128)S(1)}, u32[]{:S(2)}, u32[]{:S(2)}) collective-permute-start(f32[1,128]{1,0:T(1,128)S(1)} %slice.121), channel_id=1, source_target_pairs={{0,4},{4,8},{8,12},{12,16},{16,20},{20,24},{24,28},{1,5},{5,9},{9,... | collective-permute-start | bytes 1544 | tf_op jit(solution)/shard_map/ppermute | solution.py:28
Sparse Core Ops, SparseCore 0:
  15.0 122.2 all-reduce.20
Sparse Core Ops, SparseCore 1:
  18.0 36.8 reduce-scatter.1
  140.6 35.2 all-reduce.18
  218.7 52.6 all-reduce.22
where the time goes:
time: 332 us
  waiting for transfers between devices  181 us (55%)
  blocking collectives  48.9 us (15%)
  other arithmetic  46.8 us (14%)
  matrix products  36.4 us (11%)
  between operations  16.2 us (5%)
    psum x1, waiting for transfers between devices, local(): info = lax.psum(info_part, ('tm', 'sr'))  106 us
    psum x1, waiting for transfers between devices, local(): lax.psum((total_part, previous_part, lagged_part), 'tm')  49.8 us
    all_gather x4, blocking collectives, carried_in(): gathered = jax.tree.map(lambda a: lax.all_gather(a, axis), part)  40.2 us
    psum x1, waiting for transfers between devices, local(): proj = lax.psum(partial_value, 'sr')  25 us
    dot_general x63, matrix products, dot_high(): jnp.dot(left, right, precision=precise, preferred_element_type=jnp.float32)  22.3 us
    another operation x3, other arithmetic, local(): previous_factor = jnp.linalg.cholesky(previous)  12.4 us
    another operation x3, other arithmetic, local(): total_factor = jnp.linalg.cholesky(total)  12.4 us
    another operation x2, other arithmetic, local(): new_loadings = jax.scipy.linalg.cho_solve((total_factor, True), cross.T).T  10.6 us
  transfers between devices with their start and end apart: 5, of which 3 were waited for; matrix products, arithmetic and copies ran while one was open for 4% of the time, Pallas kernels for 0%

commit v1 on v0

--- a/solution.py
+++ b/solution.py
@@ -92,7 +92,9 @@
     )
     info_part = dot_high(loadings.T, noise_precision[:, None] * loadings)
     proj = lax.psum(partial_value, "sr")
-    info = lax.psum(info_part, ("tm", "sr"))
+    info = info_part
+    for over in ("sr", "tm"):
+        info = lax.psum(info, over)
     closed = transition - dot_high(filter_cov, dot_high(info, transition))
     inputs = dot_high(proj, filter_cov.T)
     local_filter = block_prefix(inputs, closed)

time: 332 us -> 311 us (0.937)
  waiting for transfers between devices: 181 us -> 166 us
    psum x1, waiting for transfers between devices: 106 us -> 54.8 us  [local(): info = lax.psum(info, over)]
    reduce_scatter x1, waiting for transfers between devices: 0.03 us -> 32 us  [local(): lax.psum_scatter(jnp.dot(window, scaled, preferred_element_type=jnp.float...]
    all_gather x4, blocking collectives: 40.2 us -> 36.7 us  [carried_in(): gathered = jax.tree.map(lambda a: lax.all_gather(a, axis), part)]
  transfers between devices with their start and end apart: 5 -> 5, of which waited for: 3 -> 4; matrix products, arithmetic and copies ran while one was open for 4% -> 3% of each run, Pallas kernels for 0% -> 0%
where the time goes in v1:
time: 311 us
  waiting for transfers between devices  166 us (53%)
  other arithmetic  46.8 us (15%)
  blocking collectives  45.8 us (15%)
  matrix products  34.9 us (11%)
  between operations  14.3 us (5%)
    psum x1, waiting for transfers between devices, local(): info = lax.psum(info, over)  54.8 us
    psum x1, waiting for transfers between devices, local(): lax.psum((total_part, previous_part, lagged_part), 'tm')  51.6 us
    all_gather x4, blocking collectives, carried_in(): gathered = jax.tree.map(lambda a: lax.all_gather(a, axis), part)  36.7 us
    reduce_scatter x1, waiting for transfers between devices, local(): lax.psum_scatter(jnp.dot(window, scaled, preferred_element_type=jnp.float...  32 us
    psum x1, waiting for transfers between devices, local(): proj = lax.psum(partial_value, 'sr')  27.6 us
    dot_general x63, matrix products, dot_high(): jnp.dot(left, right, precision=precise, preferred_element_type=jnp.float32)  20.7 us
    another operation x3, other arithmetic, local(): previous_factor = jnp.linalg.cholesky(previous)  12.4 us
    another operation x3, other arithmetic, local(): total_factor = jnp.linalg.cholesky(total)  12.4 us
  transfers between devices with their start and end apart: 5, of which 4 were waited for; matrix products, arithmetic and copies ran while one was open for 3% of the time, Pallas kernels for 0%

profile of v1, /device:TPU:0, one launch (start us, length us, event | category | flops | bytes accessed | tf_op | source)
XLA Modules:
  0.0 310.9 jit_solution(2182300111337458826)
XLA Ops:
  7.3 5.4 %convolution_bitcast_fusion.2 = f32[1024,128]{0,1:T(8,128)} fusion(bf16[1024,2048]{1,0:T(8,128)(2,1)} %param.12, f32[2048,128]{1,0:T(8,128)} %param.13, f32[2048]{0:T(1024)} %param.14), kind=kOutput, calls=%fused_computation.15 | convolution fusion | flops 537395200 | bytes 5775360 | tf_op jit(solution)/shard_map/dot_general | solution.py:88
  14.4 0.3 convolution_multiply_fusion
  14.9 2.8 fusion.13
  17.7 32.0 %reduce-scatter.2.cloned.1.call-done = f32[128,128]{0,1:T(8,128)} async-done(((f32[1024,128]{0,1:T(8,128)}), f32[128,128]{0,1:T(8,128)}) %reduce-scatter.2.cloned.1.call-update) | async-done | bytes 65552 | tf_op jit(solution)/shard_map/reduce_scatter | solution.py:87
  49.9 9.8 %all-gather.1 = f32[1024,128]{1,0:T(8,128)S(1)} all-gather(f32[128,128]{1,0:T(8,128)S(1)} %fusion.46), channel_id=3, replica_groups=mesh['tm'=8,'sr'=4] {'tm'}, dimensions={0}, use_global_device_ids=true | all-gather | bytes 589824 | tf_op jit(solution)/shard_map/all_gather | solution.py:13
  59.7 27.6 %all-reduce.24.cloned.1.call-done = (f32[128,128]{0,1:T(8,128)}, f32[128,128]{0,1:T(8,128)}) async-done(((f32[128,128]{0,1:T(8,128)}, f32[128,128]{0,1:T(8,128)}), (f32[128,128]{0,1:T(8,128)}, f32[128,128]{0,1:T(8,128)})) %all-reduce.24.cloned.1.call-update) | async-done | bytes 131088 | tf_op jit(solution)/shard_map/psum | solution.py:94
  87.4 1.1 fusion.124
  88.5 54.8 %all-reduce.20.cloned.1.call-done = f32[128,128]{0,1:T(8,128)} async-done(((f32[128,128]{0,1:T(8,128)}), f32[128,128]{0,1:T(8,128)}) %all-reduce.20.cloned.1.call-update) | async-done | bytes 65552 | tf_op jit(solution)/shard_map/psum | solution.py:97
  143.3 1.1 fusion.125
  144.5 0.3 fusion.16
  144.8 0.3 fusion.126
  145.5 0.3 convolution_add_fusion.12
  146.0 0.3 convolution_add_fusion.11
  146.5 0.3 convolution_add_fusion.10
  147.0 0.3 convolution_add_fusion.9
  147.4 0.3 convolution_add_fusion.8
  147.9 0.3 convolution_add_fusion.7
  148.2 8.1 %all-gather.2 = f32[8,1,128]{2,1,0:T(1,128)S(1)} all-gather(f32[1,1,128]{2,1,0:T(1,128)S(1)} %slice_bitcast_fusion.1), channel_id=1, replica_groups=mesh['tm'=8,'sr'=4] {'tm'}, dimensions={0}, use_global_device_ids=true | all-gather | bytes 4608 | tf_op jit(solution)/shard_map/all_gather | solution.py:13
  156.5 9.5 %all-gather = f32[1024,128]{1,0:T(8,128)S(1)} all-gather(f32[128,128]{1,0:T(8,128)S(1)} %fusion.47), channel_id=2, replica_groups=mesh['tm'=8,'sr'=4] {'tm'}, dimensions={0}, use_global_device_ids=true | all-gather | bytes 589824 | tf_op jit(solution)/shard_map/all_gather | solution.py:13
  166.6 0.2 fusion.73
  166.8 0.2 fusion.57
  167.6 0.2 fusion.135
  167.9 0.3 fusion.12
  168.2 0.3 convolution_add_fusion.6
  168.5 0.3 convolution_add_fusion.5
  168.7 0.3 convolution_add_fusion.4
  169.0 0.3 convolution_add_fusion.3
  169.3 0.3 convolution_add_fusion.2
  169.6 0.3 convolution_add_fusion.1
  169.9 0.3 convolution_add_fusion
  170.2 9.2 %all-gather.3 = f32[8,1,128]{2,1,0:T(1,128)S(1)} all-gather(f32[1,1,128]{2,1,0:T(1,128)S(1)} %slice_bitcast_fusion), channel_id=1, replica_groups=mesh['tm'=8,'sr'=4] {'tm'}, dimensions={0}, use_global_device_ids=true | all-gather | bytes 4608 | tf_op jit(solution)/shard_map/all_gather | solution.py:13
  179.4 1.6 while.27
  179.6 0.2 fusion.247
  179.8 0.2 fusion.247
  180.1 0.2 fusion.247
  180.3 0.2 fusion.247
  180.5 0.2 fusion.247
  180.7 0.2 fusion.247
  181.0 0.2 fusion.95
  181.2 0.2 fusion.93
  181.4 0.2 fusion.89
  181.6 0.2 fusion.79
  181.9 0.2 fusion.65
  182.7 0.2 fusion.146
  183.0 1.0 fusion.36
  184.0 0.9 fusion.147
  184.9 2.0 collective-permute-start
  186.9 9.1 %all_gather.27 = bf16[1024,128]{1,0:T(8,128)(2,1)S(1)} all-gather(bf16[128,128]{1,0:T(8,128)(2,1)S(1)} %get-tuple-element.159), channel_id=1, replica_groups=mesh['tm'=8,'sr'=4] {'tm'}, dimensions={0}, use_global_device_ids=true | all-gather | bytes 294912 | tf_op jit(solution)/shard_map/all_gather | solution.py:131
  196.0 0.9 fusion.21
  197.0 2.9 fusion.148
  199.9 51.6 %all-reduce.22.cloned.1.call-done = (f32[128,128]{0,1:T(8,128)}, f32[128,128]{0,1:T(8,128)}, f32[128,128]{0,1:T(8,128)}) async-done(((f32[128,128]{0,1:T(8,128)}, f32[128,128]{0,1:T(8,128)}, f32[128,128]{0,1:T(8,128)}), (f32[128,128]{0,1:T(8,128)}, f32[128,128]{0,1:T(8,128)}, f32[128,128]{0,1:T(8,128)})) %all-reduce.22.cloned.1.call-update) | async-done | bytes 196624 | tf_op jit(solution)/shard_map/psum | solution.py:122
  251.5 0.9 multiply_add_fusion
  252.6 11.7 %cholesky.55 = f32[128,128]{1,0:T(8,128)S(1)} custom-call(f32[128,128]{1,0:T(8,128)S(1)} %get-tuple-element.163), custom_call_target="Cholesky" | custom-call | tf_op jit(solution)/shard_map/jit(cholesky)/cholesky | solution.py:136
  264.4 0.6 compare_reduce_fusion
  265.0 0.7 fusion.20
  265.7 9.8 %custom-call.17 = f32[1,128,128]{1,2,0:T(8,128)S(1)} custom-call(f32[1,128,128]{2,1,0:T(8,128)S(1)} %fusion.20), custom_call_target="InvertDiagBlocksLowerTriangular" | custom-call | tf_op jit(solution)/shard_map/jit(_cho_solve)/triangular_solve | solution.py:137
  275.5 1.1 fusion.27
  276.6 0.9 fusion.25
  277.5 11.7 %cholesky.44 = f32[128,128]{1,0:T(8,128)S(1)} custom-call(f32[128,128]{1,0:T(8,128)S(1)} %get-tuple-element.164), custom_call_target="Cholesky" | custom-call | tf_op jit(solution)/shard_map/jit(cholesky)/cholesky | solution.py:134
  289.3 0.6 compare_reduce_fusion.1
  289.9 0.7 fusion.19
  290.6 10.0 %custom-call.16 = f32[1,128,128]{1,2,0:T(8,128)S(1)} custom-call(f32[1,128,128]{2,1,0:T(8,128)S(1)} %fusion.19), custom_call_target="InvertDiagBlocksLowerTriangular" | custom-call | tf_op jit(solution)/shard_map/jit(_cho_solve)/triangular_solve | solution.py:135
  300.5 1.1 fusion.32
  301.6 2.8 fusion.30
  (91 shorter events, 6.2 us)
Async XLA Ops:
  7.2 5.5 %copy-start = (f32[128,128]{1,0:T(8,128)S(1)}, f32[128,128]{1,0:T(8,128)}, u32[]{:S(2)}) copy-start(f32[128,128]{1,0:T(8,128)} %param.17) | copy-start | bytes 196612
  7.2 7.7 %copy-start.6 = (f32[2048]{0:T(1024)S(1)}, f32[2048]{0:T(1024)}, u32[]{:S(2)}) copy-start(f32[2048]{0:T(1024)} %param.14) | copy-start | bytes 24580
  7.2 7.7 %copy-start.1 = (f32[2048,128]{1,0:T(8,128)S(1)}, f32[2048,128]{1,0:T(8,128)}, u32[]{:S(2)}) copy-start(f32[2048,128]{1,0:T(8,128)} %param.13) | copy-start | bytes 3145732
  7.2 7.2 %copy-start.4 = (f32[128,128]{1,0:T(8,128)S(1)}, f32[128,128]{1,0:T(8,128)}, u32[]{:S(2)}) copy-start(f32[128,128]{1,0:T(8,128)} %param.18) | copy-start | bytes 196612
  7.2 7.4 %copy-start.3 = (f32[128,128]{1,0:T(8,128)S(1)}, f32[128,128]{1,0:T(8,128)}, u32[]{:S(2)}) copy-start(f32[128,128]{1,0:T(8,128)} %param.15) | copy-start | bytes 196612
  7.2 42.4 %reduce-scatter.2.cloned.1.call-start = ((), (), s32[]{:S(2)}) async-start(), calls=%async_computation.1 | async-start | bytes 589824 | tf_op jit(solution)/shard_map/reduce_scatter | solution.py:87
  12.6 74.8 %copy-start.5 = (f32[128,128]{1,0:T(8,128)S(1)}, f32[128,128]{1,0:T(8,128)}, u32[]{:S(2)}) copy-start(f32[128,128]{1,0:T(8,128)} %param.16) | copy-start | bytes 196612
  12.7 74.7 %all-reduce.24.cloned.1.call-start = ((), (), s32[]{:S(2)}) async-start(), calls=%async_computation.4 | async-start | bytes 262144 | tf_op jit(solution)/shard_map/psum | solution.py:94
  49.7 93.7 %all-reduce.20.cloned.1.call-start = ((), (), s32[]{:S(2)}) async-start(), calls=%async_computation.2 | async-start | bytes 131072 | tf_op jit(solution)/shard_map/psum | solution.py:97
  87.3 164.2 %all-reduce.22.cloned.1.call-start = ((), (), s32[]{:S(2)}) async-start(), calls=%async_computation.3 | async-start | bytes 393216 | tf_op jit(solution)/shard_map/psum | solution.py:122
  183.0 107.6 %copy-start.2 = (f32[128,128]{1,0:T(8,128)}, f32[128,128]{1,0:T(8,128)S(1)}, u32[]{:S(2)}) copy-start(f32[128,128]{1,0:T(8,128)S(1)} %get-tuple-element.160) | copy-start | bytes 196612
  184.9 11.1 %collective-permute-start = (f32[1,128]{1,0:T(1,128)S(1)}, f32[1,128]{1,0:T(1,128)S(1)}, u32[]{:S(2)}, u32[]{:S(2)}) collective-permute-start(f32[1,128]{1,0:T(1,128)S(1)} %slice.121), channel_id=1, source_target_pairs={{0,4},{4,8},{8,12},{12,16},{16,20},{20,24},{24,28},{1,5},{5,9},{9,... | collective-permute-start | bytes 1544 | tf_op jit(solution)/shard_map/ppermute | solution.py:28
Sparse Core Ops, SparseCore 0:
  12.8 36.8 reduce-scatter.1
  52.6 34.6 all-reduce.23
  90.4 52.9 all-reduce.19
  197.1 54.3 all-reduce.21
